TPU v7x, 32 devices: a whole 2x2x4 slice. The times are simulated.
32 devices in a mesh: blk: 8 (over z, x), ga: 4 (over y, core).
Axes of the slice: x: 2, y: 2, z: 4, core: 2. Of those that a mesh axis runs over, the one named last changes fastest.
Arguments:
- pair_val: bfloat16 [16, 16, 16, 2048], P('blk', None, None, 'ga'), may hold values from -0.125 to 0.125
- pair_con: bfloat16 [16, 16, 16, 2048], P('blk', None, None, 'ga'), may hold values from -6 to 6
- screened: bfloat16 [16, 2048, 2048], P('blk', None, 'ga'), may hold values from -0.125 to 0.125
- amplitude: bfloat16 [16, 16], P('blk'), may hold values from -6 to 6
- qmap: int32 [16, 16], P('blk'), may hold values from 0 to 15, as said below
Outputs:
- kernel_x: float32 [16, 16], P('blk')
Inputs may be any that keep to these rules, and one draw needn't show every extreme that they name: qmap[k, k'] is the label of the difference k - k' (periodic) on a grid of 8 by 2 points, with the points and the differences labelled at random; every row and every column holds each label once.
All inputs are finite; a program needn't handle non-finite values.
Results may differ from a plain program's by a relative error of at most 0.004.
Values may be sent and summed in bfloat16 or wider, within the bound.
A program may use at most 64 MiB of HBM per device.

v0:
```python
import functools

import jax
import jax.numpy as jnp
from jax import lax
from jax.experimental import pallas as pl
from jax.experimental.pallas import tpu as pltpu
from jax.sharding import PartitionSpec as P

NV = 4
NC = 4
ROWS = 16
TILE = 256
MESH = pl.DeviceIdType.MESH
F32 = jnp.float32
BF16 = jnp.bfloat16


def iota(shape, dim):
    return lax.broadcasted_iota(jnp.int32, shape, dim)


def one_hot(mask):
    return jnp.where(mask, 1.0, 0.0).astype(F32)


def kernel(
    blks, gas, val_hbm, con_hbm, w_hbm, amp_ref, q_ref, out_ref,
    val_in, con_in, w_in, con_send, zeta_send, con_all, zeta_all, amp_all, amp_rows, unit, contrib, fin,
    load_sem, amp_ssem, amp_rsem, con_ssem, con_rsem, zeta_ssem, zeta_rsem,
    row_ssem, row_rsem, core_ssem, core_rsem, fin_ssem, fin_rsem, hop_sem,
):
    me, ga = lax.axis_index("blk"), lax.axis_index("ga")
    local_k, total = q_ref.shape
    labels, width = w_in.shape[0], w_in.shape[2]
    wide = total * ROWS
    lane = me * gas + ga
    devices = blks * gas
    rings = gas // 2
    other = ga + 1 - 2 * (ga % 2)

    loads = [
        pltpu.make_async_copy(con_hbm, con_in, load_sem.at[0]),
        pltpu.make_async_copy(val_hbm, val_in, load_sem.at[1]),
        pltpu.make_async_copy(w_hbm, w_in, load_sem.at[2]),
    ]
    for load in loads:
        load.start()

    line = blks // 2
    z, x = me // 2, me % 2
    shifts = [(0, 1)]
    for far in range(1, line):
        shifts += [(far, 0), (-far, 0), (far, 1), (-far, 1)]
    shifts.sort(key=lambda shift: abs(shift[0]) + shift[1])

    def reach(shift):
        return abs(shift[0]) + shift[1]

    def index_of(shift):
        return (shift[0] + line - 1) * 2 + shift[1]

    def to_blk(shift):
        return (z + shift[0]) * 2 + (x + shift[1]) % 2

    def from_blk(shift):
        return (z - shift[0]) * 2 + (x + shift[1]) % 2

    def sent(chosen, action):
        for shift in chosen:
            pl.when((z + shift[0] >= 0) & (z + shift[0] < line))(functools.partial(action, shift))

    def received(chosen, action):
        for shift in chosen:
            pl.when((z - shift[0] >= 0) & (z - shift[0] < line))(functools.partial(action, shift))

    beside = jnp.minimum(z, 1) + jnp.minimum(line - 1 - z, 1)
    barrier = pltpu.get_barrier_semaphore()

    def greet(semaphore):
        for far in (1, -1):
            @pl.when((z + far >= 0) & (z + far < line))
            def _():
                pl.semaphore_signal(semaphore, inc=1, device_id=(me + 2 * far, ga), device_id_type=MESH)

    greet(barrier)
    pl.semaphore_signal(barrier, inc=1, device_id=(z * 2 + (x + 1) % 2, ga), device_id_type=MESH)
    pl.semaphore_signal(barrier, inc=1, device_id=(me, other), device_id_type=MESH)
    for hop in range(1, rings):
        pl.semaphore_signal(barrier, inc=1, device_id=(me, (ga + 2 * hop) % gas), device_id_type=MESH)

    def amp_copy(shift):
        at = index_of(shift)
        return pltpu.make_async_remote_copy(
            src_ref=amp_ref, dst_ref=amp_all.at[me],
            send_sem=amp_ssem.at[at], recv_sem=amp_rsem.at[at],
            device_id=(to_blk(shift), ga), device_id_type=MESH)

    def con_copy(shift):
        at = index_of(shift)
        return pltpu.make_async_remote_copy(
            src_ref=con_send.at[to_blk(shift)], dst_ref=con_all.at[ga, me],
            send_sem=con_ssem.at[at], recv_sem=con_rsem.at[at],
            device_id=(to_blk(shift), ga), device_id_type=MESH)

    def zeta_copy(shift):
        at = index_of(shift)
        return pltpu.make_async_remote_copy(
            src_ref=zeta_send.at[to_blk(shift)], dst_ref=zeta_all.at[me],
            send_sem=zeta_ssem.at[at], recv_sem=zeta_rsem.at[at],
            device_id=(to_blk(shift), ga), device_id_type=MESH)

    def arrival(ref, semaphores, shift):
        at = index_of(shift)
        return pltpu.make_async_remote_copy(
            src_ref=ref, dst_ref=ref, send_sem=con_ssem.at[at], recv_sem=semaphores.at[at],
            device_id=(from_blk(shift), ga), device_id_type=MESH)

    def amp_arrival(shift):
        return arrival(amp_all.at[from_blk(shift)], amp_rsem, shift)

    def con_arrival(shift):
        return arrival(con_all.at[ga, from_blk(shift)], con_rsem, shift)

    def zeta_arrival(shift):
        return arrival(zeta_all.at[from_blk(shift)], zeta_rsem, shift)

    def row_copy(hop, owner, at):
        return pltpu.make_async_remote_copy(
            src_ref=con_all.at[ga, owner], dst_ref=con_all.at[ga, owner],
            send_sem=row_ssem.at[hop, at], recv_sem=row_rsem.at[hop, at],
            device_id=(me, (ga + 2 * hop) % gas), device_id_type=MESH)

    def core_copy(hop, owner, at):
        part = (ga + gas - 2 * hop) % gas
        return pltpu.make_async_remote_copy(
            src_ref=con_all.at[part, owner], dst_ref=con_all.at[part, owner],
            send_sem=core_ssem.at[hop, at], recv_sem=core_rsem.at[hop, at],
            device_id=(me, other), device_id_type=MESH)

    def hand_on(owner, at):
        for hop in range(1, rings):
            row_copy(hop, owner, at).start()
        core_copy(0, owner, at).start()

    def across(owner, at):
        for hop in range(1, rings):
            row_copy(hop, owner, at).wait_recv()
            core_copy(hop, owner, at).start()

    def relay(shift):
        con_arrival(shift).wait_recv()
        hand_on(from_blk(shift), index_of(shift))

    spread = one_hot(iota((total, wide), 1) >> 4 == iota((total, wide), 0)).astype(BF16)
    labels_at = jnp.dot(q_ref[...].astype(F32).astype(BF16), spread, preferred_element_type=F32).astype(jnp.int32)
    row, col = iota((TILE, wide), 0), iota((TILE, wide), 1)
    same_pair = (row & 15) == (col & 15)
    same_band = ((row >> 2) & 3) == ((col >> 2) & 3)
    chunk_labels = TILE // ROWS
    chunk_blks = chunk_labels // labels

    def stored(ref, k, chunk, value):
        blocks = value.astype(BF16).reshape(chunk_blks, labels, ROWS, width)
        ref[pl.ds(chunk * chunk_blks, chunk_blks), :, pl.ds(k * ROWS, ROWS), :] = blocks

    hits = {}
    for k in range(local_k):
        for chunk in range(wide // TILE):
            hits[k, chunk] = labels_at[k : k + 1, :] == (row >> 4) + chunk * chunk_labels
    loads[0].wait()
    for k in range(local_k):
        con_k = con_in[k].reshape(wide, width)
        for chunk in range(wide // TILE):
            pick = one_hot(hits[k, chunk] & same_pair).astype(BF16)
            stored(con_send, k, chunk, jnp.dot(pick, con_k, preferred_element_type=F32))
    con_all[ga, me] = con_send[me]
    amp_all[me] = amp_ref[...]

    pl.semaphore_wait(barrier, beside + rings + 1)
    for phase in range(1, line + 1):
        if phase > 1:
            greet(hop_sem.at[phase])
            pl.semaphore_wait(hop_sem.at[phase], beside)
        near = [shift for shift in shifts if reach(shift) == phase]
        sent(near, lambda shift: amp_copy(shift).start())
        sent(near, lambda shift: con_copy(shift).start())
        if phase == 1:
            hand_on(me, 2 * line - 2)
    near = [shift for shift in shifts if reach(shift) == 1]
    rest = [shift for shift in shifts if reach(shift) > 1]
    received(near, relay)

    received(shifts, lambda shift: amp_arrival(shift).wait_recv())
    for blk in range(blks):
        amp_rows[pl.ds(blk * local_k, local_k), :] = amp_all[blk].astype(F32)
    amps = lax.dot_general(
        amp_rows[...].astype(BF16), spread, (((0,), (0,)), ((), ())), preferred_element_type=F32)
    pair, at = iota((NV * NC, wide), 0), iota((NV * NC, wide), 1)
    amps = jnp.where((pair >> 2) == (at & 3), amps, 0.0).astype(BF16)
    lines, pairs = iota((TILE, NV * NC), 0), iota((TILE, NV * NC), 1)
    amps = jnp.dot(one_hot((lines & 3) == (pairs & 3)).astype(BF16), amps, preferred_element_type=F32)
    amps = jnp.where(same_band, amps, 0.0)
    loads[1].wait()
    for k in range(local_k):
        val_k = val_in[k].reshape(wide, width)
        for chunk in range(wide // TILE):
            mix = jnp.where(hits[k, chunk], amps, 0.0).astype(BF16)
            stored(zeta_send, k, chunk, jnp.dot(mix, val_k, preferred_element_type=F32))
    zeta_all[me] = zeta_send[me]
    sent(shifts[::-1], lambda shift: zeta_copy(shift).start())

    received(rest, relay)
    across(me, 2 * line - 2)
    received(shifts, lambda shift: across(from_blk(shift), index_of(shift)))

    def gathered(owner, at):
        for hop in range(rings):
            core_copy(hop, owner, at).wait_recv()

    loads[2].wait()
    gathered(me, 2 * line - 2)
    received(shifts, lambda shift: gathered(from_blk(shift), index_of(shift)))

    group = TILE // (local_k * ROWS)
    for part in range(blks // group):
        for label in range(labels):
            summed = None
            for quarter in range(gas):
                cons = con_all[quarter, pl.ds(part * group, group), label].reshape(TILE, width)
                term = jnp.dot(cons, w_in[label, pl.ds(quarter * width, width), :], preferred_element_type=F32)
                summed = term if summed is None else summed + term
            unit[label, pl.ds(part * TILE, TILE), :] = summed.astype(BF16)

    received(shifts, lambda shift: zeta_arrival(shift).wait_recv())

    r, s = iota((TILE, TILE), 0), iota((TILE, TILE), 1)
    kept = ((r >> 4) == (s >> 4)) & ((r & 3) == (s & 3))
    c_at, w_of = iota((ROWS, 128), 0), iota((ROWS, 128), 1)
    by_c = one_hot((c_at >> 2) == (w_of & 3))
    s_at, w_at = iota((TILE, 128), 0), iota((TILE, 128), 1)
    by_v = (((s_at >> 2) & 3) == ((w_at >> 2) & 3)) & ((s_at >> 4) % local_k == (w_at >> 4))
    for part in range(blks // group):
        cross = None
        for label in range(labels):
            zetas = zeta_all[pl.ds(part * group, group), label].reshape(TILE, width)
            term = lax.dot_general(
                unit[label, pl.ds(part * TILE, TILE), :], zetas, (((1,), (1,)), ((), ())),
                preferred_element_type=F32)
            cross = term if cross is None else cross + term
        folded = jnp.sum(jnp.where(kept, cross, 0.0).reshape(TILE // ROWS, ROWS, TILE), axis=0)
        spread_c = lax.dot_general(
            folded, by_c, (((0,), (0,)), ((), ())), precision=lax.Precision.HIGHEST, preferred_element_type=F32)
        spread_c = jnp.where(by_v, spread_c, 0.0)
        per_k = jnp.sum(spread_c.reshape(group, TILE // group, 128), axis=1)
        for at in range(group):
            contrib[part * group + at] = per_k[at : at + 1]

    def fin_copy(i):
        to = (lane + i) % devices
        return pltpu.make_async_remote_copy(
            src_ref=contrib.at[to // gas], dst_ref=fin.at[i],
            send_sem=fin_ssem.at[i], recv_sem=fin_rsem.at[i],
            device_id=(to // gas, to % gas), device_id_type=MESH)

    def every(action):
        def run(i, carry):
            action(fin_copy(i))
            return carry

        lax.fori_loop(1, devices, run, 0)

    every(lambda copy: copy.start())
    fin[0] = contrib[me]

    sent(shifts, lambda shift: amp_copy(shift).wait_send())
    sent(shifts, lambda shift: con_copy(shift).wait_send())
    sent(shifts, lambda shift: zeta_copy(shift).wait_send())

    def relayed(owner, at):
        for hop in range(1, rings):
            row_copy(hop, owner, at).wait_send()
        for hop in range(rings):
            core_copy(hop, owner, at).wait_send()

    relayed(me, 2 * line - 2)
    received(shifts, lambda shift: relayed(from_blk(shift), index_of(shift)))
    every(lambda copy: copy.wait())
    total_row = jnp.sum(fin[...], axis=0) / total
    for k in range(local_k):
        out_ref[k : k + 1, :] = total_row[:, k * ROWS : (k + 1) * ROWS]


def body(pair_val, pair_con, screened, amplitude, qmap, *, blks, gas):
    local_k, total, _, width = pair_val.shape
    labels, depth, _ = screened.shape
    devices = blks * gas
    dma = pltpu.SemaphoreType.DMA
    anywhere = pl.BlockSpec(memory_space=pl.ANY)
    vmem = pl.BlockSpec(memory_space=pltpu.VMEM)
    block = (labels, local_k * ROWS, width)
    return pl.pallas_call(
        functools.partial(kernel, blks, gas),
        out_shape=jax.ShapeDtypeStruct((local_k, NV * NC), F32),
        in_specs=[anywhere, anywhere, anywhere, vmem, vmem],
        out_specs=vmem,
        scratch_shapes=[
            pltpu.VMEM(pair_val.shape, BF16),
            pltpu.VMEM(pair_con.shape, BF16),
            pltpu.VMEM(screened.shape, BF16),
            pltpu.VMEM((blks,) + block, BF16),
            pltpu.VMEM((blks,) + block, BF16),
            pltpu.VMEM((gas, blks) + block, BF16),
            pltpu.VMEM((blks,) + block, BF16),
            pltpu.VMEM((blks,) + amplitude.shape, BF16),
            pltpu.VMEM((total, NV * NC), F32),
            pltpu.VMEM((labels, total * ROWS, width), BF16),
            pltpu.VMEM((blks, 1, 128), F32),
            pltpu.VMEM((devices, 1, 128), F32),
            dma((3,)),
            *[dma((2 * blks - 2,))] * 6,
            *[dma((gas // 2, 2 * blks - 2))] * 4,
            dma((devices,)), dma((devices,)),
            pltpu.SemaphoreType.REGULAR((blks // 2 + 1,)),
        ],
        compiler_params=pltpu.CompilerParams(
            collective_id=0, has_side_effects=True, vmem_limit_bytes=60 * 1024 * 1024),
    )(pair_val, pair_con, screened, amplitude, qmap)


def solution(mesh):
    placed = (
        P("blk", None, None, "ga"),
        P("blk", None, None, "ga"),
        P("blk", None, "ga"),
        P("blk", None),
        P("blk", None),
    )
    sizes = {"blks": mesh.shape["blk"], "gas": mesh.shape["ga"]}
    return jax.shard_map(
        functools.partial(body, **sizes), mesh=mesh, in_specs=placed, out_specs=P("blk", None), check_vma=False
    )
```

profile of v0, /device:TPU:0, one launch (start us, length us, event | category | flops | bytes accessed | tf_op | source)
XLA Modules:
  0.0 39.5 jit_solution(2166468932992231309)
XLA Ops:
  0.0 38.3 %shard_map.55 = f32[2,16]{1,0:T(2,128)} custom-call(bf16[2,16,16,512]{3,2,1,0:T(8,128)(2,1)} %val_hbm.1, bf16[2,16,16,512]{3,2,1,0:T(8,128)(2,1)} %con_hbm.1, bf16[2,2048,512]{2,1,0:T(8,128)(2,1)} %w_hbm.1, bf16[2,16]{1,0:T(2,128)(2,1)} %amp_ref.1, s32[2,16]{1,0:T(2,128)} %q_ref.1), custom_call_target="tpu_custom_call" | custom-call | tf_op jit(solution)/shard_map/pallas_call | solution.py:302
  38.3 1.2 %copy.7 = f32[2,16]{1,0:T(2,128)} copy(f32[2,16]{1,0:T(2,128)} %shard_map.55) | data formatting | bytes 256
where the time goes:
time: 39.7 us; the launch traced here: 39.5 us
  Pallas kernels  38.3 us (96%)
  local copies, waits for them, and re-layouts  1.24 us (3%)
    pallas_call x1, Pallas kernels, body(): pl.pallas_call(functools.partial(kernel, blks, gas), out_shape=jax.ShapeD...  38.3 us
    unnamed x1, local copies, waits for them, and re-layouts  1.24 us

commit v1 on v0

v1 whole, which is shorter than its diff:
```python
import functools

import jax
import jax.numpy as jnp
from jax import lax
from jax.experimental import pallas as pl
from jax.experimental.pallas import tpu as pltpu
from jax.sharding import PartitionSpec as P

NV = 4
NC = 4
ROWS = 16
TILE = 256
MESH = pl.DeviceIdType.MESH
F32 = jnp.float32
BF16 = jnp.bfloat16


def iota(shape, dim):
    return lax.broadcasted_iota(jnp.int32, shape, dim)


def one_hot(mask):
    return jnp.where(mask, 1.0, 0.0).astype(F32)


def kernel(
    blks, gas, val_hbm, con_hbm, w_hbm, amp_hbm, q_hbm, out_ref,
    q_in, amp_in, val_in, con_in, w_in, con_send, zeta_send, con_all, zeta_all, amp_all, amp_rows, unit, contrib, fin,
    load_sem, amp_ssem, amp_rsem, con_ssem, con_rsem, zeta_ssem, zeta_rsem,
    row_ssem, row_rsem, core_ssem, core_rsem, fin_ssem, fin_rsem,
):
    me, ga = lax.axis_index("blk"), lax.axis_index("ga")
    local_k, total = q_in.shape
    labels, width = w_in.shape[0], w_in.shape[2]
    wide = total * ROWS
    lane = me * gas + ga
    devices = blks * gas
    rings = gas // 2
    other = ga + 1 - 2 * (ga % 2)

    barrier = pltpu.get_barrier_semaphore()
    for step in range(1, blks):
        pl.semaphore_signal(barrier, inc=1, device_id=((me + step) % blks, ga), device_id_type=MESH)
    pl.semaphore_signal(barrier, inc=1, device_id=(me, other), device_id_type=MESH)
    for hop in range(1, rings):
        pl.semaphore_signal(barrier, inc=1, device_id=(me, (ga + 2 * hop) % gas), device_id_type=MESH)

    q_load = pltpu.make_async_copy(q_hbm, q_in, load_sem.at[0])
    amp_load = pltpu.make_async_copy(amp_hbm, amp_in, load_sem.at[1])
    val_load = pltpu.make_async_copy(val_hbm, val_in, load_sem.at[2])
    w_load = pltpu.make_async_copy(w_hbm, w_in, load_sem.at[3])
    con_loads = [pltpu.make_async_copy(con_hbm.at[k], con_in.at[k], load_sem.at[4 + k]) for k in range(local_k)]
    for load in [q_load, *con_loads, amp_load, val_load, w_load]:
        load.start()

    line = blks // 2
    z, x = me // 2, me % 2

    def both(*steps):
        return [(sign * far, turn) for far in steps for turn in (1, 0) for sign in (1, -1)]

    far_first = both(*range(line - 1, 1, -1))
    con_order = both(1) + [(0, 1)] + far_first
    zeta_order = [(0, 1)] + far_first + both(1)

    def to_blk(shift):
        return (z + shift[0]) * 2 + (x + shift[1]) % 2

    def from_blk(shift):
        return (z - shift[0]) * 2 + (x + shift[1]) % 2

    def sent(chosen, action):
        for shift in chosen:
            pl.when((z + shift[0] >= 0) & (z + shift[0] < line))(functools.partial(action, shift))

    def received(chosen, action):
        for shift in chosen:
            pl.when((z - shift[0] >= 0) & (z - shift[0] < line))(functools.partial(action, shift))

    def blk_copy(src, dst, ssem, rsem, to):
        return pltpu.make_async_remote_copy(
            src_ref=src, dst_ref=dst, send_sem=ssem.at[to], recv_sem=rsem.at[me],
            device_id=(to, ga), device_id_type=MESH)

    def amp_copy(shift):
        return blk_copy(amp_in, amp_all.at[me], amp_ssem, amp_rsem, to_blk(shift))

    def con_copy(shift):
        to = to_blk(shift)
        return blk_copy(con_send.at[to], con_all.at[ga, me], con_ssem, con_rsem, to)

    def zeta_copy(shift):
        to = to_blk(shift)
        return blk_copy(zeta_send.at[to], zeta_all.at[me], zeta_ssem, zeta_rsem, to)

    def arrival(ref, ssem, rsem, owner):
        return pltpu.make_async_remote_copy(
            src_ref=ref, dst_ref=ref, send_sem=ssem.at[owner], recv_sem=rsem.at[owner],
            device_id=(owner, ga), device_id_type=MESH)

    def row_copy(hop, owner):
        return pltpu.make_async_remote_copy(
            src_ref=con_all.at[ga, owner], dst_ref=con_all.at[ga, owner],
            send_sem=row_ssem.at[hop, owner], recv_sem=row_rsem.at[hop, owner],
            device_id=(me, (ga + 2 * hop) % gas), device_id_type=MESH)

    def core_copy(hop, owner):
        part = (ga + gas - 2 * hop) % gas
        return pltpu.make_async_remote_copy(
            src_ref=con_all.at[part, owner], dst_ref=con_all.at[part, owner],
            send_sem=core_ssem.at[hop, owner], recv_sem=core_rsem.at[hop, owner],
            device_id=(me, other), device_id_type=MESH)

    def hand_on(owner):
        for hop in range(1, rings):
            row_copy(hop, owner).start()
        core_copy(0, owner).start()

    def across(owner):
        for hop in range(1, rings):
            row_copy(hop, owner).wait_recv()
            core_copy(hop, owner).start()

    def relay(shift):
        owner = from_blk(shift)
        arrival(con_all.at[ga, owner], con_ssem, con_rsem, owner).wait_recv()
        hand_on(owner)

    spread = one_hot(iota((total, wide), 1) >> 4 == iota((total, wide), 0)).astype(BF16)
    row, col = iota((TILE, wide), 0), iota((TILE, wide), 1)
    same_pair = (row & 15) == (col & 15)
    same_band = ((row >> 2) & 3) == ((col >> 2) & 3)
    chunk_labels = TILE // ROWS
    chunk_blks = chunk_labels // labels

    def stored(ref, k, chunk, value):
        blocks = value.astype(BF16).reshape(chunk_blks, labels, ROWS, width)
        ref[pl.ds(chunk * chunk_blks, chunk_blks), :, pl.ds(k * ROWS, ROWS), :] = blocks

    q_load.wait()
    labels_at = jnp.dot(q_in[...].astype(F32).astype(BF16), spread, preferred_element_type=F32).astype(jnp.int32)
    hits = {}
    for k in range(local_k):
        for chunk in range(wide // TILE):
            hits[k, chunk] = labels_at[k : k + 1, :] == (row >> 4) + chunk * chunk_labels
    for k in range(local_k):
        con_loads[k].wait()
        con_k = con_in[k].reshape(wide, width)
        for chunk in range(wide // TILE):
            pick = one_hot(hits[k, chunk] & same_pair).astype(BF16)
            stored(con_send, k, chunk, jnp.dot(pick, con_k, preferred_element_type=F32))
    amp_load.wait()

    pl.semaphore_wait(barrier, blks - 1 + rings)
    sent(con_order, lambda shift: amp_copy(shift).start())
    sent(con_order, lambda shift: con_copy(shift).start())
    con_all[ga, me] = con_send[me]
    amp_all[me] = amp_in[...]
    hand_on(me)

    received(
        con_order,
        lambda shift: arrival(amp_all.at[from_blk(shift)], amp_ssem, amp_rsem, from_blk(shift)).wait_recv())
    for blk in range(blks):
        amp_rows[pl.ds(blk * local_k, local_k), :] = amp_all[blk].astype(F32)
    amps = lax.dot_general(
        amp_rows[...].astype(BF16), spread, (((0,), (0,)), ((), ())), preferred_element_type=F32)
    pair, at = iota((NV * NC, wide), 0), iota((NV * NC, wide), 1)
    amps = jnp.where((pair >> 2) == (at & 3), amps, 0.0).astype(BF16)
    lines, pairs = iota((TILE, NV * NC), 0), iota((TILE, NV * NC), 1)
    amps = jnp.dot(one_hot((lines & 3) == (pairs & 3)).astype(BF16), amps, preferred_element_type=F32)
    amps = jnp.where(same_band, amps, 0.0)
    val_load.wait()
    for k in range(local_k):
        val_k = val_in[k].reshape(wide, width)
        for chunk in range(wide // TILE):
            mix = jnp.where(hits[k, chunk], amps, 0.0).astype(BF16)
            stored(zeta_send, k, chunk, jnp.dot(mix, val_k, preferred_element_type=F32))
    sent(zeta_order, lambda shift: zeta_copy(shift).start())
    zeta_all[me] = zeta_send[me]

    received(con_order, relay)
    across(me)
    received(con_order, lambda shift: across(from_blk(shift)))

    def gathered(owner):
        for hop in range(rings):
            core_copy(hop, owner).wait_recv()

    w_load.wait()
    for owner in range(blks):
        gathered(owner)

    block = local_k * ROWS
    group = TILE // block
    for part in range(blks // group):
        for label in range(labels):
            summed = None
            for quarter in range(gas):
                cons = con_all[quarter, pl.ds(part * group, group), label].reshape(TILE, width)
                term = jnp.dot(cons, w_in[label, pl.ds(quarter * width, width), :], preferred_element_type=F32)
                summed = term if summed is None else summed + term
            unit[pl.ds(part * group, group), label] = summed.astype(BF16).reshape(group, block, width)

    plane = 2 * block
    r, s = iota((plane, plane), 0), iota((plane, plane), 1)
    kept = ((r >> 4) == (s >> 4)) & ((r & 3) == (s & 3))
    c_at, w_of = iota((ROWS, 128), 0), iota((ROWS, 128), 1)
    by_c = one_hot((c_at >> 2) == (w_of & 3))
    s_at, w_at = iota((plane, 128), 0), iota((plane, 128), 1)
    by_v = (((s_at >> 2) & 3) == ((w_at >> 2) & 3)) & ((s_at >> 4) % local_k == (w_at >> 4))

    def fin_copy(to):
        return pltpu.make_async_remote_copy(
            src_ref=contrib.at[to // gas], dst_ref=fin.at[lane],
            send_sem=fin_ssem.at[to], recv_sem=fin_rsem.at[lane],
            device_id=(to // gas, to % gas), device_id_type=MESH)

    def finish(at):
        first = 2 * at
        for turn in range(2):
            owner = first + turn

            @pl.when(owner != me)
            def _():
                arrival(zeta_all.at[owner], zeta_ssem, zeta_rsem, owner).wait_recv()
        cross = None
        for label in range(labels):
            units = unit[pl.ds(first, 2), label].reshape(plane, width)
            zetas = zeta_all[pl.ds(first, 2), label].reshape(plane, width)
            term = lax.dot_general(units, zetas, (((1,), (1,)), ((), ())), preferred_element_type=F32)
            cross = term if cross is None else cross + term
        folded = jnp.sum(jnp.where(kept, cross, 0.0).reshape(plane // ROWS, ROWS, plane), axis=0)
        spread_c = lax.dot_general(
            folded, by_c, (((0,), (0,)), ((), ())), precision=lax.Precision.HIGHEST, preferred_element_type=F32)
        spread_c = jnp.where(by_v, spread_c, 0.0)
        contrib[pl.ds(first, 2)] = jnp.sum(spread_c.reshape(2, block, 128), axis=1, keepdims=True)
        for turn in range(2):
            for part in range(gas):
                to = (first + turn) * gas + part

                @pl.when(to != lane)
                def _():
                    fin_copy(to).start()

                @pl.when(to == lane)
                def _():
                    fin[lane] = contrib[me]

    low = z < line // 2
    near_end = jnp.where(low, z, line - 1 - z)
    finish(z)
    for step in range(line - 1):
        alone = line - 1 - 2 * near_end
        turn = step - alone
        away = near_end - turn // 2
        place = jnp.where(step < alone, line - 1 - step, near_end + away * (1 - 2 * (turn % 2)))
        finish(jnp.where(low, place, line - 1 - place))

    sent(con_order, lambda shift: amp_copy(shift).wait_send())
    sent(con_order, lambda shift: con_copy(shift).wait_send())
    sent(con_order, lambda shift: zeta_copy(shift).wait_send())
    for owner in range(blks):
        for hop in range(1, rings):
            row_copy(hop, owner).wait_send()
        for hop in range(rings):
            core_copy(hop, owner).wait_send()

    def every(i, carry):
        to = (lane + i) % devices
        fin_copy(to).wait_send()
        pltpu.make_async_remote_copy(
            src_ref=fin.at[to], dst_ref=fin.at[to], send_sem=fin_ssem.at[to], recv_sem=fin_rsem.at[to],
            device_id=(to // gas, to % gas), device_id_type=MESH).wait_recv()
        return carry

    lax.fori_loop(1, devices, every, 0)
    total_row = jnp.sum(fin[...], axis=0) / total
    for k in range(local_k):
        out_ref[k : k + 1, :] = total_row[:, k * ROWS : (k + 1) * ROWS]


def body(pair_val, pair_con, screened, amplitude, qmap, *, blks, gas):
    local_k, total, _, width = pair_val.shape
    labels, depth, _ = screened.shape
    devices = blks * gas
    dma = pltpu.SemaphoreType.DMA
    anywhere = pl.BlockSpec(memory_space=pl.ANY)
    vmem = pl.BlockSpec(memory_space=pltpu.VMEM)
    block = (labels, local_k * ROWS, width)
    return pl.pallas_call(
        functools.partial(kernel, blks, gas),
        out_shape=pltpu.VMEM((local_k, NV * NC), F32),
        in_specs=[anywhere] * 5,
        out_specs=vmem,
        scratch_shapes=[
            pltpu.VMEM(qmap.shape, jnp.int32),
            pltpu.VMEM(amplitude.shape, BF16),
            pltpu.VMEM(pair_val.shape, BF16),
            pltpu.VMEM(pair_con.shape, BF16),
            pltpu.VMEM(screened.shape, BF16),
            pltpu.VMEM((blks,) + block, BF16),
            pltpu.VMEM((blks,) + block, BF16),
            pltpu.VMEM((gas, blks) + block, BF16),
            pltpu.VMEM((blks,) + block, BF16),
            pltpu.VMEM((blks,) + amplitude.shape, BF16),
            pltpu.VMEM((total, NV * NC), F32),
            pltpu.VMEM((blks,) + block, BF16),
            pltpu.VMEM((blks, 1, 128), F32),
            pltpu.VMEM((devices, 1, 128), F32),
            dma((4 + local_k,)),
            *[dma((blks,))] * 6,
            *[dma((gas // 2, blks))] * 4,
            dma((devices,)), dma((devices,)),
        ],
        compiler_params=pltpu.CompilerParams(
            collective_id=0, has_side_effects=True, vmem_limit_bytes=60 * 1024 * 1024),
    )(pair_val, pair_con, screened, amplitude, qmap)


def solution(mesh):
    placed = (
        P("blk", None, None, "ga"),
        P("blk", None, None, "ga"),
        P("blk", None, "ga"),
        P("blk", None),
        P("blk", None),
    )
    sizes = {"blks": mesh.shape["blk"], "gas": mesh.shape["ga"]}
    return jax.shard_map(
        functools.partial(body, **sizes), mesh=mesh, in_specs=placed, out_specs=P("blk", None), check_vma=False
    )
```

time: 39.7 us -> 38.2 us (0.962)
  Pallas kernels: 38.3 us -> 37.5 us
  local copies, waits for them, and re-layouts: 1.24 us -> 0.56 us
    pallas_call x1, Pallas kernels: 38.3 us -> 37.5 us  [body(): pl.pallas_call(functools.partial(kernel, blks, gas), out_shape=pltpu.VMEM...]
    unnamed x1, local copies, waits for them, and re-layouts: 1.24 us -> 0.56 us
where the time goes in v1:
time: 38.2 us; the launch traced here: 38.1 us
  Pallas kernels  37.5 us (98%)
  local copies, waits for them, and re-layouts  0.56 us (1%)
    pallas_call x1, Pallas kernels, body(): pl.pallas_call(functools.partial(kernel, blks, gas), out_shape=pltpu.VMEM...  37.5 us

profile of v1, /device:TPU:0, one launch (start us, length us, event | category | flops | bytes accessed | tf_op | source)
XLA Modules:
  0.0 38.1 jit_solution(11252462825352130323)
XLA Ops:
  0.0 37.5 %shard_map.55 = f32[2,16]{1,0:T(2,128)S(1)} custom-call(bf16[2,16,16,512]{3,2,1,0:T(8,128)(2,1)} %val_hbm.1, bf16[2,16,16,512]{3,2,1,0:T(8,128)(2,1)} %con_hbm.1, bf16[2,2048,512]{2,1,0:T(8,128)(2,1)} %w_hbm.1, bf16[2,16]{1,0:T(2,128)(2,1)} %amp_hbm.1, s32[2,16]{1,0:T(2,128)} %q_hbm.1), custom_call_target="tpu_custom_call" | custom-call | tf_op jit(solution)/shard_map/pallas_call | solution.py:292
  37.5 0.6 %copy.7 = f32[2,16]{1,0:T(2,128)} copy(f32[2,16]{1,0:T(2,128)S(1)} %shard_map.55) | data formatting | bytes 256

commit v2 on v1

v2 whole, which is shorter than its diff:
```python
import functools

import jax
import jax.numpy as jnp
from jax import lax
from jax.experimental import pallas as pl
from jax.experimental.pallas import tpu as pltpu
from jax.sharding import PartitionSpec as P

NV = 4
NC = 4
ROWS = 16
TILE = 256
LANES = 128
MESH = pl.DeviceIdType.MESH
F32 = jnp.float32
BF16 = jnp.bfloat16


def iota(shape, dim):
    return lax.broadcasted_iota(jnp.int32, shape, dim)


def one_hot(mask):
    return jnp.where(mask, 1.0, 0.0).astype(F32)


def kernel(
    blks, gas, val_hbm, con_hbm, w_hbm, amp_hbm, q_hbm, out_ref,
    q_in, amp_in, val_in, con_in, w_in, con_send, zeta_send, con_all, zeta_all, amp_all, amp_rows, unit, contrib, fin,
    load_sem, send_sem, amp_rsem, con_rsem, zeta_rsem, row_rsem, core_rsem, fin_rsem,
):
    me, ga = lax.axis_index("blk"), lax.axis_index("ga")
    local_k, total = q_in.shape
    labels, width = w_in.shape[0], w_in.shape[2]
    wide = total * ROWS
    lane = me * gas + ga
    devices = blks * gas
    rings = gas // 2
    other = ga + 1 - 2 * (ga % 2)

    barrier = pltpu.get_barrier_semaphore()
    for step in range(1, blks):
        pl.semaphore_signal(barrier, inc=1, device_id=((me + step) % blks, ga), device_id_type=MESH)
    pl.semaphore_signal(barrier, inc=1, device_id=(me, other), device_id_type=MESH)
    for hop in range(1, rings):
        pl.semaphore_signal(barrier, inc=1, device_id=(me, (ga + 2 * hop) % gas), device_id_type=MESH)

    q_load = pltpu.make_async_copy(q_hbm, q_in, load_sem.at[0])
    amp_load = pltpu.make_async_copy(amp_hbm, amp_in, load_sem.at[1])
    val_load = pltpu.make_async_copy(val_hbm, val_in, load_sem.at[2])
    w_load = pltpu.make_async_copy(w_hbm, w_in, load_sem.at[3])
    con_loads = [pltpu.make_async_copy(con_hbm.at[k], con_in.at[k], load_sem.at[4 + k]) for k in range(local_k)]
    for load in [q_load, *con_loads, amp_load]:
        load.start()

    line = blks // 2
    z, x = me // 2, me % 2

    def both(*steps):
        return [(sign * far, turn) for far in steps for turn in (1, 0) for sign in (1, -1)]

    far_first = both(*range(line - 1, 1, -1))
    near = both(1) + [(0, 1)]
    con_order = near + far_first
    zeta_order = [(0, 1)] + far_first + both(1)

    def to_blk(shift):
        return (z + shift[0]) * 2 + (x + shift[1]) % 2

    def from_blk(shift):
        return (z - shift[0]) * 2 + (x + shift[1]) % 2

    def sent(chosen, action):
        for shift in chosen:
            pl.when((z + shift[0] >= 0) & (z + shift[0] < line))(functools.partial(action, shift))

    def received(chosen, action):
        for shift in chosen:
            pl.when((z - shift[0] >= 0) & (z - shift[0] < line))(functools.partial(action, shift))

    def blk_copy(src, dst, ssem, rsem, to):
        return pltpu.make_async_remote_copy(
            src_ref=src, dst_ref=dst, send_sem=ssem, recv_sem=rsem, device_id=(to, ga), device_id_type=MESH)

    def amp_copy(shift):
        return blk_copy(amp_in, amp_all.at[me], send_sem.at[0], amp_rsem, to_blk(shift))

    def con_copy(shift):
        to = to_blk(shift)
        return blk_copy(con_send.at[to], con_all.at[ga, me], send_sem.at[1], con_rsem.at[me], to)

    def zeta_copy(shift):
        to = to_blk(shift)
        return blk_copy(zeta_send.at[to], zeta_all.at[me], send_sem.at[2], zeta_rsem.at[me], to)

    def awaited(ref, sem):
        return pltpu.make_async_remote_copy(
            src_ref=ref, dst_ref=ref, send_sem=sem, recv_sem=sem, device_id=(me, other), device_id_type=MESH)

    def row_copy(hop, owner):
        return pltpu.make_async_remote_copy(
            src_ref=con_all.at[ga, owner], dst_ref=con_all.at[ga, owner],
            send_sem=send_sem.at[3], recv_sem=row_rsem.at[hop - 1, owner],
            device_id=(me, (ga + 2 * hop) % gas), device_id_type=MESH)

    def core_copy(hop, owner):
        part = (ga + gas - 2 * hop) % gas
        return pltpu.make_async_remote_copy(
            src_ref=con_all.at[part, owner], dst_ref=con_all.at[part, owner],
            send_sem=send_sem.at[4], recv_sem=core_rsem.at[owner // (blks // 2)],
            device_id=(me, other), device_id_type=MESH)

    def hand_on(owner):
        for hop in range(1, rings):
            row_copy(hop, owner).start()
        core_copy(0, owner).start()

    def across(owner):
        for hop in range(1, rings):
            row_copy(hop, owner).wait_recv()
            core_copy(hop, owner).start()

    def relay(shift):
        owner = from_blk(shift)
        awaited(con_all.at[ga, owner], con_rsem.at[owner]).wait_recv()
        hand_on(owner)

    spread = one_hot(iota((total, wide), 1) >> 4 == iota((total, wide), 0)).astype(BF16)
    row, col = iota((TILE, wide), 0), iota((TILE, wide), 1)
    same_pair = (row & 15) == (col & 15)
    same_band = ((row >> 2) & 3) == ((col >> 2) & 3)
    chunk_labels = TILE // ROWS
    chunk_blks = chunk_labels // labels

    def stored(ref, k, chunk, value):
        blocks = value.astype(BF16).reshape(chunk_blks, labels, ROWS, width)
        ref[pl.ds(chunk * chunk_blks, chunk_blks), :, pl.ds(k * ROWS, ROWS), :] = blocks

    q_load.wait()
    labels_at = jnp.dot(q_in[...].astype(F32).astype(BF16), spread, preferred_element_type=F32).astype(jnp.int32)
    hits = {}
    for k in range(local_k):
        for chunk in range(wide // TILE):
            hits[k, chunk] = labels_at[k : k + 1, :] == (row >> 4) + chunk * chunk_labels
    for k in range(local_k):
        con_loads[k].wait()
        con_k = con_in[k].reshape(wide, width)
        for chunk in range(wide // TILE):
            pick = one_hot(hits[k, chunk] & same_pair).astype(BF16)
            stored(con_send, k, chunk, jnp.dot(pick, con_k, preferred_element_type=F32))
    amp_load.wait()
    val_load.start()
    w_load.start()

    pl.semaphore_wait(barrier, blks - 1 + rings)
    sent(con_order, lambda shift: amp_copy(shift).start())
    sent(con_order, lambda shift: con_copy(shift).start())
    con_all[ga, me] = con_send[me]
    amp_all[me] = amp_in[...]
    hand_on(me)

    received(near, relay)

    awaited(amp_all.at[pl.ds(0, blks - 1)], amp_rsem).wait_recv()
    for blk in range(blks):
        amp_rows[pl.ds(blk * local_k, local_k), :] = amp_all[blk].astype(F32)
    amps = lax.dot_general(
        amp_rows[...].astype(BF16), spread, (((0,), (0,)), ((), ())), preferred_element_type=F32)
    pair, at = iota((NV * NC, wide), 0), iota((NV * NC, wide), 1)
    amps = jnp.where((pair >> 2) == (at & 3), amps, 0.0).astype(BF16)
    lines, pairs = iota((TILE, NV * NC), 0), iota((TILE, NV * NC), 1)
    amps = jnp.dot(one_hot((lines & 3) == (pairs & 3)).astype(BF16), amps, preferred_element_type=F32)
    amps = jnp.where(same_band, amps, 0.0)
    val_load.wait()
    for k in range(local_k):
        val_k = val_in[k].reshape(wide, width)
        for chunk in range(wide // TILE):
            mix = jnp.where(hits[k, chunk], amps, 0.0).astype(BF16)
            stored(zeta_send, k, chunk, jnp.dot(mix, val_k, preferred_element_type=F32))
    inner = (z > 0) & (z < line - 1)

    @pl.when(inner)
    def _():
        sent(zeta_order, lambda shift: zeta_copy(shift).start())

    zeta_all[me] = zeta_send[me]

    across(me)
    received(near, lambda shift: across(from_blk(shift)))
    received(far_first, relay)

    @pl.when(jnp.logical_not(inner))
    def _():
        sent(zeta_order, lambda shift: zeta_copy(shift).start())


    block = local_k * ROWS
    half = blks // 2
    group = min(half, TILE // block)
    low = z < line // 2

    def gathered(which):
        awaited(con_all.at[pl.ds(0, rings), pl.ds(0, half)], core_rsem.at[which]).wait_recv()
        for part in range(half // group):
            first = which * half + part * group
            for label in range(labels):
                summed = None
                for quarter in range(gas):
                    cons = con_all[quarter, pl.ds(first, group), label].reshape(group * block, width)
                    term = jnp.dot(cons, w_in[label, pl.ds(quarter * width, width), :], preferred_element_type=F32)
                    summed = term if summed is None else summed + term
                unit[pl.ds(first, group), label] = summed.astype(BF16).reshape(group, block, width)

    far_half = jnp.where(low, 1, 0)
    received(far_first, lambda shift: across(from_blk(shift)))
    w_load.wait()
    gathered(1 - far_half)
    gathered(far_half)

    def fin_copy(to):
        return pltpu.make_async_remote_copy(
            src_ref=contrib.at[to // gas], dst_ref=fin.at[lane],
            send_sem=send_sem.at[5], recv_sem=fin_rsem,
            device_id=(to // gas, to % gas), device_id_type=MESH)

    def finish(first, count):
        for turn in range(count):
            owner = first + turn

            @pl.when(owner != me)
            def _():
                awaited(zeta_all.at[owner], zeta_rsem.at[owner]).wait_recv()
        rows = count * block
        r, s = iota((rows, rows), 0), iota((rows, rows), 1)
        kept = ((r >> 4) == (s >> 4)) & ((r & 3) == (s & 3))
        cross = None
        for label in range(labels):
            units = unit[pl.ds(first, count), label].reshape(rows, width)
            zetas = zeta_all[pl.ds(first, count), label].reshape(rows, width)
            term = lax.dot_general(units, zetas, (((1,), (1,)), ((), ())), preferred_element_type=F32)
            cross = term if cross is None else cross + term
        folded = jnp.sum(jnp.where(kept, cross, 0.0).reshape(rows // ROWS, ROWS, rows), axis=0)
        if rows < LANES:
            folded = jnp.concatenate([folded, jnp.zeros((ROWS, LANES - rows), F32)], axis=1)
        lanes = iota((ROWS, LANES), 1)
        for step in (1, 2):
            folded = folded + jnp.where(
                (lanes & step) == 0, pltpu.roll(folded, LANES - step, 1), pltpu.roll(folded, step, 1))
        mine = jnp.sum(jnp.where((iota((ROWS, LANES), 0) >> 2) == (lanes & 3), folded, 0.0), axis=0, keepdims=True)
        for turn in range(count):
            contrib[first + turn] = mine if turn == 0 else pltpu.roll(mine, LANES - turn * block, 1)
        for turn in range(count):
            for part in range(gas):
                to = (first + turn) * gas + part

                @pl.when(to != lane)
                def _():
                    fin_copy(to).start()

                @pl.when(to == lane)
                def _():
                    fin[lane] = contrib[me]

    wave = LANES // block
    for step in range(line // 2):
        if step == line // 2 - 1:
            for at in range(half // wave):
                finish((1 - far_half) * half + at * wave, wave)
        finish(2 * jnp.where(low, line - 1 - step, step), 2)

    awaited(amp_all.at[pl.ds(0, blks - 1)], send_sem.at[0]).wait_send()
    awaited(con_send.at[pl.ds(0, blks - 1)], send_sem.at[1]).wait_send()
    awaited(zeta_send.at[pl.ds(0, blks - 1)], send_sem.at[2]).wait_send()
    awaited(con_all.at[pl.ds(0, rings - 1)], send_sem.at[3]).wait_send()
    awaited(con_all.at[pl.ds(0, rings)], send_sem.at[4]).wait_send()
    awaited(fin.at[pl.ds(0, devices - 1)], send_sem.at[5]).wait_send()
    awaited(fin.at[pl.ds(0, devices - 1)], fin_rsem).wait_recv()
    total_row = jnp.sum(fin[...], axis=0) / total
    for k in range(local_k):
        out_ref[k : k + 1, :] = total_row[:, k * ROWS : (k + 1) * ROWS]


def body(pair_val, pair_con, screened, amplitude, qmap, *, blks, gas):
    local_k, total, _, width = pair_val.shape
    labels, depth, _ = screened.shape
    devices = blks * gas
    dma = pltpu.SemaphoreType.DMA
    anywhere = pl.BlockSpec(memory_space=pl.ANY)
    vmem = pl.BlockSpec(memory_space=pltpu.VMEM)
    block = (labels, local_k * ROWS, width)
    return pl.pallas_call(
        functools.partial(kernel, blks, gas),
        out_shape=pltpu.VMEM((local_k, NV * NC), F32),
        in_specs=[anywhere] * 5,
        out_specs=vmem,
        scratch_shapes=[
            pltpu.VMEM(qmap.shape, jnp.int32),
            pltpu.VMEM(amplitude.shape, BF16),
            pltpu.VMEM(pair_val.shape, BF16),
            pltpu.VMEM(pair_con.shape, BF16),
            pltpu.VMEM(screened.shape, BF16),
            pltpu.VMEM((blks,) + block, BF16),
            pltpu.VMEM((blks,) + block, BF16),
            pltpu.VMEM((gas, blks) + block, BF16),
            pltpu.VMEM((blks,) + block, BF16),
            pltpu.VMEM((blks,) + amplitude.shape, BF16),
            pltpu.VMEM((total, NV * NC), F32),
            pltpu.VMEM((blks,) + block, BF16),
            pltpu.VMEM((blks, 1, 128), F32),
            pltpu.VMEM((devices, 1, 128), F32),
            dma((4 + local_k,)),
            dma((6,)), dma, dma((blks,)), dma((blks,)), dma((gas // 2 - 1, blks)), dma((2,)), dma,
        ],
        compiler_params=pltpu.CompilerParams(
            collective_id=0, has_side_effects=True, vmem_limit_bytes=60 * 1024 * 1024),
    )(pair_val, pair_con, screened, amplitude, qmap)


def solution(mesh):
    placed = (
        P("blk", None, None, "ga"),
        P("blk", None, None, "ga"),
        P("blk", None, "ga"),
        P("blk", None),
        P("blk", None),
    )
    sizes = {"blks": mesh.shape["blk"], "gas": mesh.shape["ga"]}
    return jax.shard_map(
        functools.partial(body, **sizes), mesh=mesh, in_specs=placed, out_specs=P("blk", None), check_vma=False
    )
```

time: 38.2 us -> 33.4 us (0.87)
  Pallas kernels: 37.5 us -> 32.7 us
    pallas_call x1, Pallas kernels: 37.5 us -> 32.7 us  [body(): pl.pallas_call(functools.partial(kernel, blks, gas), out_shape=pltpu.VMEM...]
where the time goes in v2:
time: 33.4 us; the launch traced here: 33.3 us
  Pallas kernels  32.7 us (98%)
  local copies, waits for them, and re-layouts  0.56 us (2%)
    pallas_call x1, Pallas kernels, body(): pl.pallas_call(functools.partial(kernel, blks, gas), out_shape=pltpu.VMEM...  32.7 us

profile of v2, /device:TPU:0, one launch (start us, length us, event | category | flops | bytes accessed | tf_op | source)
XLA Modules:
  0.0 33.3 jit_solution(5146237688509090157)
XLA Ops:
  0.0 32.7 %shard_map.55 = f32[2,16]{1,0:T(2,128)S(1)} custom-call(bf16[2,16,16,512]{3,2,1,0:T(8,128)(2,1)} %val_hbm.1, bf16[2,16,16,512]{3,2,1,0:T(8,128)(2,1)} %con_hbm.1, bf16[2,2048,512]{2,1,0:T(8,128)(2,1)} %w_hbm.1, bf16[2,16]{1,0:T(2,128)(2,1)} %amp_hbm.1, s32[2,16]{1,0:T(2,128)} %q_hbm.1), custom_call_target="tpu_custom_call" | custom-call | tf_op jit(solution)/shard_map/pallas_call | solution.py:292
  32.7 0.6 %copy.7 = f32[2,16]{1,0:T(2,128)} copy(f32[2,16]{1,0:T(2,128)S(1)} %shard_map.55) | data formatting | bytes 256

commit v3 on v2

--- a/solution.py
+++ b/solution.py
@@ -28,7 +28,7 @@
 def kernel(
     blks, gas, val_hbm, con_hbm, w_hbm, amp_hbm, q_hbm, out_ref,
     q_in, amp_in, val_in, con_in, w_in, con_send, zeta_send, con_all, zeta_all, amp_all, amp_rows, unit, contrib, fin,
-    load_sem, send_sem, amp_rsem, con_rsem, zeta_rsem, row_rsem, core_rsem, fin_rsem,
+    load_sem, hop_sem, send_sem, amp_rsem, con_rsem, zeta_rsem, row_rsem, core_rsem, fin_rsem,
 ):
     me, ga = lax.axis_index("blk"), lax.axis_index("ga")
     local_k, total = q_in.shape
@@ -38,13 +38,23 @@
     devices = blks * gas
     rings = gas // 2
     other = ga + 1 - 2 * (ga % 2)
-
+    line = blks // 2
+    z, x = me // 2, me % 2
+    beside = jnp.minimum(z, 1) + jnp.minimum(line - 1 - z, 1)
     barrier = pltpu.get_barrier_semaphore()
-    for step in range(1, blks):
-        pl.semaphore_signal(barrier, inc=1, device_id=((me + step) % blks, ga), device_id_type=MESH)
+
+    def greet(semaphore):
+        for far in (1, -1):
+            @pl.when((z + far >= 0) & (z + far < line))
+            def _():
+                pl.semaphore_signal(semaphore, inc=1, device_id=(me + 2 * far, ga), device_id_type=MESH)
+
+    greet(barrier)
+    pl.semaphore_signal(barrier, inc=1, device_id=(z * 2 + (x + 1) % 2, ga), device_id_type=MESH)
     pl.semaphore_signal(barrier, inc=1, device_id=(me, other), device_id_type=MESH)
     for hop in range(1, rings):
         pl.semaphore_signal(barrier, inc=1, device_id=(me, (ga + 2 * hop) % gas), device_id_type=MESH)
+
 
     q_load = pltpu.make_async_copy(q_hbm, q_in, load_sem.at[0])
     amp_load = pltpu.make_async_copy(amp_hbm, amp_in, load_sem.at[1])
@@ -54,9 +64,6 @@
     for load in [q_load, *con_loads, amp_load]:
         load.start()
 
-    line = blks // 2
-    z, x = me // 2, me % 2
-
     def both(*steps):
         return [(sign * far, turn) for far in steps for turn in (1, 0) for sign in (1, -1)]
 
@@ -121,8 +128,17 @@
             row_copy(hop, owner).wait_recv()
             core_copy(hop, owner).start()
 
-    def relay(shift):
-        owner = from_blk(shift)
+    half = blks // 2
+    low = z < line // 2
+    far_half = jnp.where(low, 1, 0)
+    mine = [(1 - far_half) * half + at for at in range(half)]
+    theirs = [2 * jnp.where(low, line - 1 - at // 2, at // 2) + at % 2 for at in range(half)]
+
+    def others(owners, action):
+        for owner in owners:
+            pl.when(owner != me)(functools.partial(action, owner))
+
+    def relay(owner):
         awaited(con_all.at[ga, owner], con_rsem.at[owner]).wait_recv()
         hand_on(owner)
 
@@ -153,14 +169,38 @@
     val_load.start()
     w_load.start()
 
-    pl.semaphore_wait(barrier, blks - 1 + rings)
-    sent(con_order, lambda shift: amp_copy(shift).start())
-    sent(con_order, lambda shift: con_copy(shift).start())
-    con_all[ga, me] = con_send[me]
-    amp_all[me] = amp_in[...]
-    hand_on(me)
-
-    received(near, relay)
+    pl.semaphore_wait(barrier, beside + rings + 1)
+    inner = (z > 0) & (z < line - 1)
+    turned = [shift for shift in con_order if shift[1] == 1 and shift[0] != 0]
+
+    def straight(far):
+        return [(far, 0), (-far, 0)] if far < line else []
+
+    for phase in range(1, line + 1):
+        if phase > 1:
+            pl.semaphore_wait(hop_sem.at[phase - 2], beside)
+        if phase < line:
+            greet(hop_sem.at[phase - 1])
+        reached = [shift for shift in con_order if abs(shift[0]) + shift[1] == phase]
+        sent(reached, lambda shift: amp_copy(shift).start())
+        if phase == 1:
+            sent(reached, lambda shift: con_copy(shift).start())
+        else:
+            sent(straight(phase), lambda shift: pl.when(inner)(con_copy(shift).start))
+        if phase == 2:
+            sent([(1, 1), (-1, 1)], lambda shift: pl.when(jnp.logical_not(inner))(con_copy(shift).start))
+        if phase == line - 1:
+            sent(turned, lambda shift: pl.when(inner)(con_copy(shift).start))
+        if phase == line:
+            for far in range(line - 1, 1, -1):
+                sent(straight(far), lambda shift: pl.when(jnp.logical_not(inner))(con_copy(shift).start))
+            sent(turned[2:], lambda shift: pl.when(jnp.logical_not(inner))(con_copy(shift).start))
+        if phase == 1:
+            con_all[ga, me] = con_send[me]
+            amp_all[me] = amp_in[...]
+            hand_on(me)
+
+    others(mine, relay)
 
     awaited(amp_all.at[pl.ds(0, blks - 1)], amp_rsem).wait_recv()
     for blk in range(blks):
@@ -178,27 +218,24 @@
         for chunk in range(wide // TILE):
             mix = jnp.where(hits[k, chunk], amps, 0.0).astype(BF16)
             stored(zeta_send, k, chunk, jnp.dot(mix, val_k, preferred_element_type=F32))
-    inner = (z > 0) & (z < line - 1)
-
-    @pl.when(inner)
-    def _():
-        sent(zeta_order, lambda shift: zeta_copy(shift).start())
-
+    def crosses(shift):
+        return (z + shift[0] >= line // 2) == low
+
+    def zeta_start(held, shift):
+        pl.when(jnp.logical_not(inner | jnp.logical_not(crosses(shift))) == held)(zeta_copy(shift).start)
+
+    sent(zeta_order, functools.partial(zeta_start, False))
     zeta_all[me] = zeta_send[me]
 
     across(me)
-    received(near, lambda shift: across(from_blk(shift)))
-    received(far_first, relay)
-
-    @pl.when(jnp.logical_not(inner))
-    def _():
-        sent(zeta_order, lambda shift: zeta_copy(shift).start())
-
+    others(mine, across)
+    for owner in theirs:
+        relay(owner)
+
+    sent(zeta_order, functools.partial(zeta_start, True))
 
     block = local_k * ROWS
-    half = blks // 2
     group = min(half, TILE // block)
-    low = z < line // 2
 
     def gathered(which):
         awaited(con_all.at[pl.ds(0, rings), pl.ds(0, half)], core_rsem.at[which]).wait_recv()
@@ -212,8 +249,8 @@
                     summed = term if summed is None else summed + term
                 unit[pl.ds(first, group), label] = summed.astype(BF16).reshape(group, block, width)
 
-    far_half = jnp.where(low, 1, 0)
-    received(far_first, lambda shift: across(from_blk(shift)))
+    for owner in theirs:
+        across(owner)
     w_load.wait()
     gathered(1 - far_half)
     gathered(far_half)
@@ -310,7 +347,7 @@
             pltpu.VMEM((blks, 1, 128), F32),
             pltpu.VMEM((devices, 1, 128), F32),
             dma((4 + local_k,)),
-            dma((6,)), dma, dma((blks,)), dma((blks,)), dma((gas // 2 - 1, blks)), dma((2,)), dma,
+            pltpu.SemaphoreType.REGULAR((max(blks // 2 - 1, 1),)), dma((6,)), dma, dma((blks,)), dma((blks,)), dma((gas // 2 - 1, blks)), dma((2,)), dma,
         ],
         compiler_params=pltpu.CompilerParams(
             collective_id=0, has_side_effects=True, vmem_limit_bytes=60 * 1024 * 1024),

time: 33.4 us -> 32.5 us (0.973)
  Pallas kernels: 32.7 us -> 31.7 us
    pallas_call x1, Pallas kernels: 32.7 us -> 31.7 us  [body(): pl.pallas_call(functools.partial(kernel, blks, gas), out_shape=pltpu.VMEM...]
where the time goes in v3:
time: 32.5 us; the launch traced here: 32.3 us
  Pallas kernels  31.7 us (98%)
  local copies, waits for them, and re-layouts  0.56 us (2%)
    pallas_call x1, Pallas kernels, body(): pl.pallas_call(functools.partial(kernel, blks, gas), out_shape=pltpu.VMEM...  31.7 us

profile of v3, /device:TPU:0, one launch (start us, length us, event | category | flops | bytes accessed | tf_op | source)
XLA Modules:
  0.0 32.3 jit_solution(16655708022219536850)
XLA Ops:
  0.0 31.7 %shard_map.55 = f32[2,16]{1,0:T(2,128)S(1)} custom-call(bf16[2,16,16,512]{3,2,1,0:T(8,128)(2,1)} %val_hbm.1, bf16[2,16,16,512]{3,2,1,0:T(8,128)(2,1)} %con_hbm.1, bf16[2,2048,512]{2,1,0:T(8,128)(2,1)} %w_hbm.1, bf16[2,16]{1,0:T(2,128)(2,1)} %amp_hbm.1, s32[2,16]{1,0:T(2,128)} %q_hbm.1), custom_call_target="tpu_custom_call" | custom-call | tf_op jit(solution)/shard_map/pallas_call | solution.py:329
  31.8 0.6 %copy.7 = f32[2,16]{1,0:T(2,128)} copy(f32[2,16]{1,0:T(2,128)S(1)} %shard_map.55) | data formatting | bytes 256
